TPU v7x, 8 devices: a whole 2x2x1 slice. The times are simulated.
8 devices in a mesh: dp: 1 (over z), sp: 8 (over y, x, core).
Axes of the slice: x: 2, y: 2, z: 1, core: 2. Of those that a mesh axis runs over, the one named last changes fastest.
Arguments:
- x_in: bfloat16 [2, 8192, 384], P('dp', 'sp')
- grad_y: bfloat16 [2, 8192, 384], P('dp', 'sp')
- ln_gain: float32 [384], replicated
- ln_bias: float32 [384], replicated
- w_qkv: bfloat16 [384, 1152], replicated
- w_out: bfloat16 [384, 384], replicated
- temp_tau: float32 [8], replicated
Outputs:
- output 1: bfloat16 [2, 8192, 384], P('dp', 'sp')
- output 2: bfloat16 [2, 8192, 384], P('dp', 'sp')
- output 3: bfloat16 [384, 1152], P(('dp', 'sp'))
- output 4: bfloat16 [384, 384], P(('dp', 'sp'))
- output 5: float32 [384], P('dp')
- output 6: float32 [384], P('dp')
- output 7: float32 [8], P('dp')
All inputs are finite; a program needn't handle non-finite values.
Results may differ from a plain program's by a relative error of at most 0.00912741.
Values are sent between devices in bfloat16 or wider.
A program may use at most 1 GiB of HBM per device.

v0:
```python
import functools

import jax
import jax.numpy as jnp
from jax import lax
from jax.experimental import pallas as pl
from jax.experimental.pallas import tpu as pltpu
from jax.sharding import PartitionSpec as P

LN_EPS = 1e-6
MESH = pl.DeviceIdType.MESH
KERNEL_VMEM = 63713280
F32 = jnp.float32
BF16 = jnp.bfloat16
LANES = 128
G_ROWS = 32
P_ROWS = 24
BACK_ROWS = 32
SPLIT = 3


def dot(a, b, ca, cb):
    return lax.dot_general(a, b, (((ca,), (cb,)), ((), ())), preferred_element_type=F32)


def roll(val, amount):
    amount = amount % LANES
    return pltpu.roll(val, amount, 1) if amount else val


def scope(name):
    return jax.named_scope(name)


def body(images, tokens, dim, heads, n,
         x_hbm, dy_hbm, gain_hbm, bias_hbm, wqkv_hbm, wout_hbm, tau_hbm,
         y_v, dx_v, gwqkv_ref, gwout_ref, sums_ref,
         x_v, dy_v, gain_v, bias_v, tau_v, wqkv_v, wout_v, xhat_v, rstd_v, du_v, u_v, qkv_v, do_v, o_v, dqkv_v,
         g_send, g_recv, p_send, p_recv, back_a, back_g, bd_a, bd_g, cq_v, ck_v,
         part, pair_recv, chip_sum, x_recv, y_recv, x_send2, y_send2, x_recv2, y_recv2, ln_all,
         load_sem, g_ssem, g_rsem, p_ssem, p_rsem, a_ssem, a_rsem, d_ssem, d_rsem,
         pair_ssem, pair_rsem, st_ssem, st_rsem, ln_ssem, ln_rsem):
    hd = dim // heads
    half = hd // 2
    tiles = dim // LANES
    me = lax.axis_index("sp")
    core = lax.rem(me, 2)
    chip = me // 2
    px = lax.rem(chip, 2)
    py = chip // 2
    partner = me + 1 - 2 * core
    dev_x = me + 2 - 4 * px
    dev_y = me + 4 - 8 * py

    def dev(d):
        return {"sp": d}

    def rows(b):
        return pl.ds(pl.multiple_of(b * tokens, tokens), tokens)

    def load_x(b):
        return pltpu.make_async_copy(x_hbm.at[b], x_v.at[rows(b)], load_sem.at[b])

    def load_dy(b):
        return pltpu.make_async_copy(dy_hbm.at[b], dy_v.at[rows(b)], load_sem.at[images + b])

    load_wqkv = pltpu.make_async_copy(wqkv_hbm, wqkv_v, load_sem.at[2 * images])
    load_wout = pltpu.make_async_copy(wout_hbm, wout_v, load_sem.at[2 * images + 1])
    load_gain = pltpu.make_async_copy(gain_hbm, gain_v, load_sem.at[2 * images + 2])
    load_bias = pltpu.make_async_copy(bias_hbm, bias_v, load_sem.at[2 * images + 3])
    load_tau = pltpu.make_async_copy(tau_hbm, tau_v, load_sem.at[2 * images + 4])
    load_x(0).start()
    load_gain.start()
    load_bias.start()
    load_wqkv.start()
    load_x(1).start()
    load_wout.start()
    load_dy(0).start()
    load_dy(1).start()
    load_tau.start()

    barrier = pltpu.get_barrier_semaphore()
    for off in range(1, n):
        pl.semaphore_signal(barrier, inc=1, device_id=dev(lax.rem(me + off, n)), device_id_type=MESH)

    lane = lax.broadcasted_iota(jnp.int32, (hd, LANES), 1)
    row = lax.broadcasted_iota(jnp.int32, (hd, LANES), 0)

    def pieces(h):
        base = 0 if h < SPLIT else LANES
        first = h * hd - base
        found = []
        for t in range(2):
            lo, hi = max(first, t * LANES), min(first + hd, (t + 1) * LANES)
            if lo < hi:
                found.append((t, lo - t * LANES, hi - t * LANES))
        return (0 if h < SPLIT else 1), first, found

    def head_block(blocks, h):
        which, first, found = pieces(h)
        total = None
        for t, lo, hi in found:
            tile = blocks[which][first:first + hd, t * LANES:(t + 1) * LANES]
            tile = jnp.where((lane >= lo) & (lane < hi), tile, 0.0)
            total = tile if total is None else total + tile
        return total

    def head_row(vec, h):
        total = None
        for t in range(tiles):
            lo, hi = max(h * hd, t * LANES), min((h + 1) * hd, (t + 1) * LANES)
            if lo < hi:
                mask = (lane[0:1, :] >= lo - t * LANES) & (lane[0:1, :] < hi - t * LANES)
                tile = jnp.where(mask, vec[:, t * LANES:(t + 1) * LANES], 0.0)
                total = tile if total is None else total + tile
        return total

    def pack(val, s):
        return roll(val[0:half, :], -s) + roll(val[half:hd, :], 64 - s)

    def unpack(val):
        return jnp.concatenate([val, roll(val, 64)], axis=0)

    def exchange(send, recv, ssem, rsem, b, off):
        dst = lax.rem(me + off, n)
        return pltpu.make_async_remote_copy(
            src_ref=send.at[b, dst], dst_ref=recv.at[b, off - 1],
            send_sem=ssem.at[b, off - 1], recv_sem=rsem.at[b, off - 1],
            device_id=dev(dst), device_id_type=MESH)

    def g_copy(b, off):
        return exchange(g_send, g_recv, g_ssem, g_rsem, b, off)

    def p_copy(b, off):
        return exchange(p_send, p_recv, p_ssem, p_rsem, b, off)

    def spread(buf, ssem, rsem, b, off, src):
        return pltpu.make_async_remote_copy(
            src_ref=buf.at[b, src], dst_ref=buf.at[b, src],
            send_sem=ssem.at[b, off - 1], recv_sem=rsem.at[b, off - 1],
            device_id=dev(lax.rem(me + off, n)), device_id_type=MESH)

    def a_copy(b, off):
        return spread(back_a, a_ssem, a_rsem, b, off, me)

    def a_arrival(b, off):
        return spread(back_a, a_ssem, a_rsem, b, off, lax.rem(me + n - off, n))

    def d_copy(b, off):
        return spread(back_g, d_ssem, d_rsem, b, off, me)

    def d_arrival(b, off):
        return spread(back_g, d_ssem, d_rsem, b, off, lax.rem(me + n - off, n))

    def phase_g(b, carry):
        rs = rows(b)
        load_x(b).wait()

        @pl.when(b == 0)
        def _():
            load_gain.wait()
            load_bias.wait()
            load_wqkv.wait()

        gain = gain_v[...].reshape(1, dim)
        bias = bias_v[...].reshape(1, dim)
        xf = x_v[rs, :].astype(F32)
        mean = jnp.mean(xf, axis=-1, keepdims=True)
        cent = xf - mean
        rstd = lax.rsqrt(jnp.mean(cent * cent, axis=-1, keepdims=True) + LN_EPS)
        xhat = cent * rstd
        xhat_v[rs, :] = xhat
        rstd_v[rs, :] = rstd
        u = (xhat * gain + bias).astype(BF16)
        u_v[rs, :] = u
        qkv_v[rs, :] = dot(u, wqkv_v[...], 1, 0).astype(BF16)
        q = qkv_v[rs, 0:dim]
        k = qkv_v[rs, dim:2 * dim]
        gram = (dot(q[:, 0:256], k[:, 0:256], 0, 0), dot(q[:, 128:384], k[:, 128:384], 0, 0))
        qf = q.astype(F32)
        kf = k.astype(F32)
        ssq = jnp.sum(qf * qf, axis=0, keepdims=True)
        ssk = jnp.sum(kf * kf, axis=0, keepdims=True)
        for h in range(heads):
            s = (h * hd) % LANES
            g_send[b, h, 0:half, :] = pack(head_block(gram, h), s)
            qk = jnp.concatenate([head_row(ssq, h), head_row(ssk, h), jnp.zeros((6, LANES), F32)], axis=0)
            g_send[b, h, half:G_ROWS, :] = roll(qk, -s)

        @pl.when(b == 0)
        def _():
            pl.semaphore_wait(barrier, n - 1)

        for off in range(1, n):
            g_copy(b, off).start()
        return carry

    def phase_p(b, carry):
        rs = rows(b)

        @pl.when(b == 0)
        def _():
            load_wout.wait()

        load_dy(b).wait()
        do = dot(dy_v[rs, :], wout_v[...], 1, 1).astype(BF16)
        do_v[rs, :] = do
        v = qkv_v[rs, 2 * dim:3 * dim]
        dprob = (dot(do[:, 0:256], v[:, 0:256], 0, 0), dot(do[:, 128:384], v[:, 128:384], 0, 0))
        for h in range(heads):
            p_send[b, h] = pack(head_block(dprob, h), (h * hd) % LANES)
        for off in range(1, n):
            p_copy(b, off).start()
        return carry

    with scope("phase_g"):
        lax.fori_loop(0, images, phase_g, 0)
    with scope("phase_p"):
        lax.fori_loop(0, images, phase_p, 0)

    load_tau.wait()
    tau = tau_v[me]
    eye = lane == row
    live = lane < hd
    live1 = live[0:1, :]

    def owner_a(b):
        with scope("wait_g"):
            for off in range(1, n):
                g_copy(b, off).wait_recv()
        total = g_send[b, me]
        for off in range(1, n):
            total = total + g_recv[b, off - 1]
        gram = unpack(total[0:half, :])
        ssq = total[half:half + 1, :]
        ssk = total[half + 1:half + 2, :]
        rq_col = jnp.sum(jnp.where(eye, lax.rsqrt(ssq), 0.0), axis=1, keepdims=True)
        scale = jnp.where(live, tau * rq_col * lax.rsqrt(ssk), 0.0)
        logits = jnp.where(live, gram * scale, 0.0)
        top = jnp.max(jnp.where(live, logits, -jnp.inf), axis=1, keepdims=True)
        e = jnp.where(live, jnp.exp(logits - top), 0.0)
        p = e / jnp.sum(e, axis=1, keepdims=True)
        back_a[b, me] = jnp.concatenate([pack(p, 0), jnp.zeros((BACK_ROWS - half, LANES), F32)], axis=0).astype(BF16)
        for off in range(1, n):
            a_copy(b, off).start()
        return p, logits, scale, ssq, ssk

    def owner_g(b, state):
        p, logits, scale, ssq, ssk = state
        with scope("wait_p"):
            for off in range(1, n):
                p_copy(b, off).wait_recv()
        total = p_send[b, me]
        for off in range(1, n):
            total = total + p_recv[b, off - 1]
        dprob = jnp.where(live, unpack(total), 0.0).astype(BF16).astype(F32)
        glog = p * (dprob - jnp.sum(p * dprob, axis=1, keepdims=True))
        weighted = glog * logits
        w_row = jnp.sum(weighted, axis=1, keepdims=True)
        cq = -jnp.sum(jnp.where(eye, w_row, 0.0), axis=0, keepdims=True)
        cq = jnp.where(live1, cq / ssq, 0.0)
        ck = jnp.where(live1, -jnp.sum(weighted, axis=0, keepdims=True) / ssk, 0.0)
        c_row = jnp.broadcast_to(cq + roll(ck, 64), (BACK_ROWS - half, LANES))
        back_g[b, me] = jnp.concatenate([pack(glog * scale, 0), c_row], axis=0).astype(BF16)
        for off in range(1, n):
            d_copy(b, off).start()
        return jnp.sum(w_row, axis=0, keepdims=True)

    def build(b, got_of, arrival, bd, name):
        with scope(name):
            for off in range(1, n):
                arrival(b, off).wait_recv()
        tails = []
        for h in range(heads):
            got = got_of[b, h].astype(F32)
            which, first, found = pieces(h)
            s = first % LANES
            low = roll(got[0:half, :], s)
            high = roll(got[0:half, :], s + 64)
            val = jnp.concatenate([low, high], axis=0)
            cols = [jnp.zeros((hd, LANES), F32) for _ in range(2)]
            for t, lo, hi in found:
                cols[t] = jnp.where((lane >= lo) & (lane < hi), val, 0.0)
            bd[b, which, first:first + hd, :] = jnp.concatenate(cols, axis=1).astype(BF16)
            tails.append(got[half:half + 1, :])
        return tails

    def clear(bd):
        for b in range(images):
            bd[b, 0, SPLIT * hd:256, :] = jnp.zeros((256 - SPLIT * hd, 256), BF16)
            bd[b, 1, 0:SPLIT * hd - LANES, :] = jnp.zeros((SPLIT * hd - LANES, 256), BF16)

    def build_a(b):
        build(b, back_a, a_arrival, bd_a, "wait_a")

    def build_g(b):
        tails = build(b, back_g, d_arrival, bd_g, "wait_d")
        for dst, shift in ((cq_v, 0), (ck_v, 64)):
            vec = [jnp.zeros((1, LANES), F32) for _ in range(tiles)]
            for h in range(heads):
                val = roll(tails[h], shift + h * hd)
                for t in range(tiles):
                    lo, hi = max(h * hd, t * LANES), min((h + 1) * hd, (t + 1) * LANES)
                    if lo < hi:
                        mask = (lane[0:1, :] >= lo - t * LANES) & (lane[0:1, :] < hi - t * LANES)
                        vec[t] = vec[t] + jnp.where(mask, val, 0.0)
            dst[b] = jnp.broadcast_to(jnp.concatenate(vec, axis=1), (8, dim))

    def per_head(tok, mats, transposed):
        c = 1 if transposed else 0
        left = dot(tok[:, 0:256], mats[0], 1, c)
        right = dot(tok[:, 128:384], mats[1], 1, c)
        return jnp.concatenate([left[:, 0:128], left[:, 128:256] + right[:, 0:128], right[:, 128:256]], axis=1)

    def pair_copy(c):
        return pltpu.make_async_remote_copy(
            src_ref=part.at[c, :, :, 1 - core], dst_ref=pair_recv.at[c],
            send_sem=pair_ssem.at[c], recv_sem=pair_rsem.at[c],
            device_id=dev(partner), device_id_type=MESH)

    def stage_copies(c, stage):
        if stage == 0:
            refs = ((chip_sum.at[c, :, 1 - px, 0], x_recv.at[c], dev_x),
                    (chip_sum.at[c, 1 - py, :, 1], y_recv.at[c], dev_y))
        else:
            refs = ((x_send2.at[c], x_recv2.at[c], dev_x), (y_send2.at[c], y_recv2.at[c], dev_y))
        return [pltpu.make_async_remote_copy(
            src_ref=src, dst_ref=dst, send_sem=st_ssem.at[c, stage, i], recv_sem=st_rsem.at[c, stage, i],
            device_id=dev(d), device_id_type=MESH) for i, (src, dst, d) in enumerate(refs)]

    def rs0(c, value):
        part[c] = value.reshape(2, 2, 2, 2, half, dim)
        pair_copy(c).start()

    def rs1(c):
        with scope("wait_pair"):
            pair_copy(c).wait_recv()
        chip_sum[c] = part[c, :, :, core] + pair_recv[c]
        for copy in stage_copies(c, 0):
            copy.start()

    def rs2(c):
        with scope("wait_st0"):
            for copy in stage_copies(c, 0):
                copy.wait_recv()
        x_send2[c] = chip_sum[c, py, 1 - px, 1] + y_recv[c, 1 - px]
        y_send2[c] = chip_sum[c, 1 - py, px, 0] + x_recv[c, 1 - py]
        for copy in stage_copies(c, 1):
            copy.start()

    def rs3(c):
        own_a = chip_sum[c, py, px, 0] + x_recv[c, py]
        own_b = chip_sum[c, py, px, 1] + y_recv[c, px]
        with scope("wait_st1"):
            for copy in stage_copies(c, 1):
                copy.wait_recv()
        return jnp.concatenate([own_a + y_recv2[c], own_b + x_recv2[c]], axis=0).astype(BF16)

    def heads_out(b):
        rs = rows(b)
        o_v[rs, :] = per_head(qkv_v[rs, 2 * dim:3 * dim], bd_a[b], True).astype(BF16)

    def grad_v(b):
        rs = rows(b)
        dqkv_v[rs, 2 * dim:3 * dim] = per_head(do_v[rs, :], bd_a[b], False).astype(BF16)

    def grad_q(b):
        rs = rows(b)
        q = qkv_v[rs, 0:dim]
        k = qkv_v[rs, dim:2 * dim]
        dqkv_v[rs, 0:dim] = (per_head(k, bd_g[b], True) + cq_v[b, 0:1, :] * q.astype(F32)).astype(BF16)

    def grad_k(b):
        rs = rows(b)
        q = qkv_v[rs, 0:dim]
        k = qkv_v[rs, dim:2 * dim]
        dqkv_v[rs, dim:2 * dim] = (per_head(q, bd_g[b], False) + ck_v[b, 0:1, :] * k.astype(F32)).astype(BF16)

    def out_y(b):
        rs = rows(b)
        y_v[rs, :] = (x_v[rs, :].astype(F32) + dot(o_v[rs, :], wout_v[...], 1, 0)).astype(BF16)

    def grad_u(b):
        rs = rows(b)
        du = dot(dqkv_v[rs, :], wqkv_v[...], 1, 1).astype(BF16)
        du_v[rs, :] = du
        du = du.astype(F32)
        return jnp.sum(du * xhat_v[rs, :], axis=0, keepdims=True), jnp.sum(du, axis=0, keepdims=True)

    def out_dx(b):
        rs = rows(b)
        gain = gain_v[...].reshape(1, dim)
        xhat = xhat_v[rs, :]
        a = du_v[rs, :].astype(F32) * gain
        ma = jnp.mean(a, axis=-1, keepdims=True)
        mx = jnp.mean(a * xhat, axis=-1, keepdims=True)
        dx_v[rs, :] = (dy_v[rs, :].astype(F32) + rstd_v[rs, :] * (a - ma - xhat * mx)).astype(BF16)

    clear(bd_a)
    clear(bd_g)
    with scope("owner_a0"):
        state0 = owner_a(0)
    with scope("owner_a1"):
        state1 = owner_a(1)
    with scope("owner_g0"):
        w0 = owner_g(0, state0)
    build_a(0)
    with scope("heads_out"):
        heads_out(0)
    with scope("grad_v"):
        grad_v(0)
    with scope("owner_g1"):
        w1 = owner_g(1, state1)
    build_a(1)
    with scope("heads_out"):
        heads_out(1)
    with scope("part0"):
        rs0(0, dot(o_v[...], dy_v[...], 0, 0))
    with scope("grad_v"):
        grad_v(1)
    with scope("part1"):
        rs0(1, dot(u_v[...], dqkv_v[:, 2 * dim:3 * dim], 0, 0))
    rs1(0)
    build_g(0)
    with scope("grad_q"):
        grad_q(0)
    build_g(1)
    with scope("grad_q"):
        grad_q(1)
    rs1(1)
    with scope("part2"):
        rs0(2, dot(u_v[...], dqkv_v[:, 0:dim], 0, 0))
    with scope("grad_k"):
        grad_k(0)
    with scope("grad_k"):
        grad_k(1)
    rs1(2)
    with scope("part3"):
        rs0(3, dot(u_v[...], dqkv_v[:, dim:2 * dim], 0, 0))
    rs2(0)
    with scope("grad_u"):
        sg0, sb0 = grad_u(0)
    rs1(3)
    rs2(1)
    with scope("grad_u"):
        sg1, sb1 = grad_u(1)

    sg = sg0 + sg1
    sb = sb0 + sb1
    st = jnp.where(lane[0:1, :] == me, (w0 + w1) / tau, 0.0)
    ln_rows = [val[:, t * LANES:(t + 1) * LANES] for val in (sg, sb) for t in range(tiles)]
    ln_all[me] = jnp.concatenate(ln_rows + [st, jnp.zeros((1, LANES), F32)], axis=0)

    def ln_copy(off, src):
        return pltpu.make_async_remote_copy(
            src_ref=ln_all.at[src], dst_ref=ln_all.at[src],
            send_sem=ln_ssem.at[off - 1], recv_sem=ln_rsem.at[off - 1],
            device_id=dev(lax.rem(me + off, n)), device_id_type=MESH)

    for off in range(1, n):
        ln_copy(off, me).start()

    rs2(2)
    with scope("out_dx"):
        out_dx(0)
    with scope("out_y"):
        out_y(0)
    rs2(3)
    with scope("out_dx"):
        out_dx(1)
    with scope("out_y"):
        out_y(1)
    gwout_ref[...] = rs3(0)
    gwqkv_ref[:, 2 * dim:3 * dim] = rs3(1)
    gwqkv_ref[:, 0:dim] = rs3(2)
    gwqkv_ref[:, dim:2 * dim] = rs3(3)
    with scope("wait_ln"):
        for off in range(1, n):
            ln_copy(off, lax.rem(me + n - off, n)).wait_recv()
    sums = ln_all[0]
    for d in range(1, n):
        sums = sums + ln_all[d]
    sums_ref[...] = sums

    with scope("final"):
        for b in range(images):
            for off in range(1, n):
                g_copy(b, off).wait_send()
                p_copy(b, off).wait_send()
                a_copy(b, off).wait_send()
                d_copy(b, off).wait_send()
        for c in range(4):
            pair_copy(c).wait_send()
            for stage in range(2):
                for copy in stage_copies(c, stage):
                    copy.wait_send()
        for off in range(1, n):
            ln_copy(off, me).wait_send()


def finish(dim, heads, y_v, dx_v, gwqkv_v, gwout_v, sums_v,
           y_hbm, dx_hbm, gwqkv_hbm, gwout_hbm, ggain_ref, gbias_ref, gtau_ref, sem):
    pairs = ((y_v, y_hbm), (dx_v, dx_hbm), (gwqkv_v, gwqkv_hbm), (gwout_v, gwout_hbm))
    copies = [pltpu.make_async_copy(src, dst, sem.at[i]) for i, (src, dst) in enumerate(pairs)]
    for copy in copies:
        copy.start()
    tiles = dim // LANES
    for t in range(tiles):
        ggain_ref[t * LANES:(t + 1) * LANES] = sums_v[t, :]
        gbias_ref[t * LANES:(t + 1) * LANES] = sums_v[tiles + t, :]
    gtau_ref[...] = sums_v[2 * tiles, 0:heads]
    for copy in copies:
        copy.wait()


def solution(mesh):
    n = mesh.shape["sp"]

    def local_step(x_in, grad_y, ln_gain, ln_bias, w_qkv, w_out, temp_tau):
        images, tokens, dim = x_in.shape
        heads = temp_tau.shape[0]
        hd = dim // heads
        half = hd // 2
        num = images * tokens
        hbm = pl.BlockSpec(memory_space=pltpu.HBM)
        vmem = pl.BlockSpec(memory_space=pltpu.VMEM)
        dma = pltpu.SemaphoreType.DMA
        params = pltpu.CompilerParams(collective_id=0, has_side_effects=True, vmem_limit_bytes=KERNEL_VMEM)
        y, dx, gwqkv, gwout, sums = pl.pallas_call(
            functools.partial(body, images, tokens, dim, heads, n),
            out_shape=(
                pltpu.VMEM((num, dim), BF16),
                pltpu.VMEM((num, dim), BF16),
                pltpu.VMEM((hd, 3 * dim), BF16),
                pltpu.VMEM((hd, dim), BF16),
                pltpu.VMEM((8, LANES), F32),
            ),
            in_specs=[hbm] * 7,
            out_specs=(vmem, vmem, vmem, vmem, vmem),
            scratch_shapes=[
                pltpu.VMEM((num, dim), BF16),
                pltpu.VMEM((num, dim), BF16),
                pltpu.VMEM((dim,), F32),
                pltpu.VMEM((dim,), F32),
                pltpu.SMEM((heads,), F32),
                pltpu.VMEM((dim, 3 * dim), BF16),
                pltpu.VMEM((dim, dim), BF16),
                pltpu.VMEM((num, dim), F32),
                pltpu.VMEM((num, 1), F32),
                pltpu.VMEM((num, dim), BF16),
                pltpu.VMEM((num, dim), BF16),
                pltpu.VMEM((num, 3 * dim), BF16),
                pltpu.VMEM((num, dim), BF16),
                pltpu.VMEM((num, dim), BF16),
                pltpu.VMEM((num, 3 * dim), BF16),
                pltpu.VMEM((images, heads, G_ROWS, LANES), F32),
                pltpu.VMEM((images, n - 1, G_ROWS, LANES), F32),
                pltpu.VMEM((images, heads, P_ROWS, LANES), F32),
                pltpu.VMEM((images, n - 1, P_ROWS, LANES), F32),
                pltpu.VMEM((images, heads, BACK_ROWS, LANES), BF16),
                pltpu.VMEM((images, heads, BACK_ROWS, LANES), BF16),
                pltpu.VMEM((images, 2, 256, 256), BF16),
                pltpu.VMEM((images, 2, 256, 256), BF16),
                pltpu.VMEM((images, 8, dim), F32),
                pltpu.VMEM((images, 8, dim), F32),
                pltpu.VMEM((4, 2, 2, 2, 2, half, dim), F32),
                pltpu.VMEM((4, 2, 2, 2, half, dim), F32),
                pltpu.VMEM((4, 2, 2, 2, half, dim), F32),
                pltpu.VMEM((4, 2, half, dim), F32),
                pltpu.VMEM((4, 2, half, dim), F32),
                pltpu.VMEM((4, half, dim), F32),
                pltpu.VMEM((4, half, dim), F32),
                pltpu.VMEM((4, half, dim), F32),
                pltpu.VMEM((4, half, dim), F32),
                pltpu.VMEM((n, 8, LANES), F32),
                dma((2 * images + 5,)),
                dma((images, n - 1)), dma((images, n - 1)),
                dma((images, n - 1)), dma((images, n - 1)),
                dma((images, n - 1)), dma((images, n - 1)),
                dma((images, n - 1)), dma((images, n - 1)),
                dma((4,)), dma((4,)),
                dma((4, 2, 2)), dma((4, 2, 2)),
                dma((n - 1,)), dma((n - 1,)),
            ],
            compiler_params=params,
            name="xca_step",
        )(x_in, grad_y, ln_gain, ln_bias, w_qkv, w_out, temp_tau)
        y, dx, gwqkv, gwout, ggain, gbias, gtau = pl.pallas_call(
            functools.partial(finish, dim, heads),
            out_shape=(
                jax.ShapeDtypeStruct((num, dim), BF16),
                jax.ShapeDtypeStruct((num, dim), BF16),
                jax.ShapeDtypeStruct((hd, 3 * dim), BF16),
                jax.ShapeDtypeStruct((hd, dim), BF16),
                jax.ShapeDtypeStruct((dim,), F32),
                jax.ShapeDtypeStruct((dim,), F32),
                jax.ShapeDtypeStruct((heads,), F32),
            ),
            in_specs=[vmem] * 5,
            out_specs=(hbm, hbm, hbm, hbm, vmem, vmem, vmem),
            scratch_shapes=[dma((4,))],
            compiler_params=pltpu.CompilerParams(vmem_limit_bytes=2**20),
            name="xca_finish",
        )(y, dx, gwqkv, gwout, sums)
        return y.reshape(x_in.shape), dx.reshape(x_in.shape), gwqkv, gwout, ggain, gbias, gtau

    token_spec = P("dp", "sp", None)
    return jax.shard_map(local_step, mesh=mesh, in_specs=(token_spec, token_spec, P(), P(), P(), P(), P()), out_specs=(token_spec, token_spec, P(("dp", "sp"), None), P(("dp", "sp"), None), P("dp"), P("dp"), P("dp")), check_vma=False)
```

profile of v0, /device:TPU:0, one launch (start us, length us, event | category | flops | bytes accessed | tf_op | source)
XLA Modules:
  0.0 37.4 jit_solution(18122220712006487827)
XLA Ops:
  0.6 34.3 %xca_step.1 = (bf16[2048,384]{1,0:T(8,128)(2,1)S(1)}, bf16[2048,384]{1,0:T(8,128)(2,1)S(1)}, bf16[48,1152]{1,0:T(8,128)(2,1)S(1)}, bf16[48,384]{1,0:T(8,128)(2,1)S(1)}, f32[8,128]{1,0:T(8,128)S(1)}) custom-call(bf16[2,1024,384]{2,1,0:T(8,128)(2,1)} %x_hbm.1, bf16[2,1024,384]{2,1,0:T(8,128)(2,1)} %dy_hbm.1, f32[384]{0:T(512)} %gain_hbm.1, f32[384]{0:T(512)} %bias_hbm.1, ...), custom_call_target="tpu_custom_call" | custom-call | tf_op jit(solution)/shard_map/xca_step/pallas_call | solution.py:529
  34.9 2.3 %xca_finish.1 = (bf16[2048,384]{1,0:T(8,128)(2,1)}, bf16[2048,384]{1,0:T(8,128)(2,1)}, bf16[48,1152]{1,0:T(8,128)(2,1)}, bf16[48,384]{1,0:T(8,128)(2,1)}, f32[384]{0:T(512)}, /*index=5*/f32[384]{0:T(512)}, f32[8]{0:T(128)}) custom-call(bf16[2048,384]{1,0:T(8,128)(2,1)S(1)} %get-tuple-element.19.y_v, bf16[2048,384]{1,0:T(8,128)(2,1)S(1)} %get-tuple-element.20.dx_v, ...), custom_call_target="tpu_custom_call" | custom-call | tf_op jit(solution)/shard_map/xca_finish/pallas_call | solution.py:588
where the time goes:
time: 37.5 us; the launch traced here: 37.4 us
  Pallas kernels  36.6 us (98%)
  between operations  0.8 us (2%)
    pallas_call x1, Pallas kernels, local_step(): pl.pallas_call(functools.partial(body, images, tokens, dim, heads, n), ou...  34.3 us
    pallas_call x1, Pallas kernels, local_step(): pl.pallas_call(functools.partial(finish, dim, heads), out_shape=(jax.Shap...  2.29 us

commit v1 on v0

--- a/solution.py
+++ b/solution.py
@@ -13,9 +13,10 @@
 F32 = jnp.float32
 BF16 = jnp.bfloat16
 LANES = 128
-G_ROWS = 32
+G_ROWS = 24
 P_ROWS = 24
-BACK_ROWS = 32
+BACK_ROWS = 24
+STARTS = (0, 384, 768, 1152, 1408, 1536)
 SPLIT = 3
 
 
@@ -35,8 +36,8 @@
 def body(images, tokens, dim, heads, n,
          x_hbm, dy_hbm, gain_hbm, bias_hbm, wqkv_hbm, wout_hbm, tau_hbm,
          y_v, dx_v, gwqkv_ref, gwout_ref, sums_ref,
-         x_v, dy_v, gain_v, bias_v, tau_v, wqkv_v, wout_v, xhat_v, rstd_v, du_v, u_v, qkv_v, do_v, o_v, dqkv_v,
-         g_send, g_recv, p_send, p_recv, back_a, back_g, bd_a, bd_g, cq_v, ck_v,
+         x_v, dy_v, gain_v, bias_v, tau_v, wqkv_v, wout_v, xhat_v, rstd_v, du_v, u_v, ut_v, qkv_v, do_v, o_v, dqkv_v,
+         g_send, g_recv, p_send, p_recv, back_a, back_g, bd_a, bd_g, c_v,
          part, pair_recv, chip_sum, x_recv, y_recv, x_send2, y_send2, x_recv2, y_recv2, ln_all,
          load_sem, g_ssem, g_rsem, p_ssem, p_rsem, a_ssem, a_rsem, d_ssem, d_rsem,
          pair_ssem, pair_rsem, st_ssem, st_rsem, ln_ssem, ln_rsem):
@@ -64,16 +65,19 @@
     def load_dy(b):
         return pltpu.make_async_copy(dy_hbm.at[b], dy_v.at[rows(b)], load_sem.at[images + b])
 
-    load_wqkv = pltpu.make_async_copy(wqkv_hbm, wqkv_v, load_sem.at[2 * images])
-    load_wout = pltpu.make_async_copy(wout_hbm, wout_v, load_sem.at[2 * images + 1])
+    load_w = [pltpu.make_async_copy(wqkv_hbm.at[:, pl.ds((i + 2) % 3 * dim, dim)], wqkv_v.at[:, pl.ds(i * dim, dim)],
+                                    load_sem.at[2 * images + 5 + i]) for i in range(3)]
+    load_wout = pltpu.make_async_copy(wout_hbm, wout_v, load_sem.at[2 * images])
     load_gain = pltpu.make_async_copy(gain_hbm, gain_v, load_sem.at[2 * images + 2])
     load_bias = pltpu.make_async_copy(bias_hbm, bias_v, load_sem.at[2 * images + 3])
     load_tau = pltpu.make_async_copy(tau_hbm, tau_v, load_sem.at[2 * images + 4])
     load_x(0).start()
     load_gain.start()
     load_bias.start()
-    load_wqkv.start()
+    load_w[1].start()
+    load_w[2].start()
     load_x(1).start()
+    load_w[0].start()
     load_wout.start()
     load_dy(0).start()
     load_dy(1).start()
@@ -96,6 +100,8 @@
                 found.append((t, lo - t * LANES, hi - t * LANES))
         return (0 if h < SPLIT else 1), first, found
 
+    side = (lane[0:8, :] >= hd) & (lane[0:8, :] < hd + 16)
+
     def head_block(blocks, h):
         which, first, found = pieces(h)
         total = None
@@ -121,6 +127,9 @@
     def unpack(val):
         return jnp.concatenate([val, roll(val, 64)], axis=0)
 
+    def beside(val, s):
+        return jnp.concatenate([jnp.where(side, roll(val, hd - 16 * i - s), 0.0) for i in range(3)], axis=0)
+
     def exchange(send, recv, ssem, rsem, b, off):
         dst = lax.rem(me + off, n)
         return pltpu.make_async_remote_copy(
@@ -152,16 +161,8 @@
     def d_arrival(b, off):
         return spread(back_g, d_ssem, d_rsem, b, off, lax.rem(me + n - off, n))
 
-    def phase_g(b, carry):
-        rs = rows(b)
-        load_x(b).wait()
-
-        @pl.when(b == 0)
-        def _():
-            load_gain.wait()
-            load_bias.wait()
-            load_wqkv.wait()
-
+    def layer_norm(b):
+        rs = rows(b)
         gain = gain_v[...].reshape(1, dim)
         bias = bias_v[...].reshape(1, dim)
         xf = x_v[rs, :].astype(F32)
@@ -171,11 +172,21 @@
         xhat = cent * rstd
         xhat_v[rs, :] = xhat
         rstd_v[rs, :] = rstd
-        u = (xhat * gain + bias).astype(BF16)
-        u_v[rs, :] = u
-        qkv_v[rs, :] = dot(u, wqkv_v[...], 1, 0).astype(BF16)
-        q = qkv_v[rs, 0:dim]
-        k = qkv_v[rs, dim:2 * dim]
+        u_v[rs, :] = (xhat * gain + bias).astype(BF16)
+
+    def project_qk(b):
+        for i in range(2):
+            rs = pl.ds(b * tokens + i * (tokens // 2), tokens // 2)
+            qkv_v[rs, dim:3 * dim] = dot(u_v[rs, :], wqkv_v[:, dim:3 * dim], 1, 0).astype(BF16)
+
+    def project_v(b):
+        rs = rows(b)
+        qkv_v[rs, 0:dim] = dot(u_v[rs, :], wqkv_v[:, 0:dim], 1, 0).astype(BF16)
+
+    def gram_part(b):
+        rs = rows(b)
+        q = qkv_v[rs, dim:2 * dim]
+        k = qkv_v[rs, 2 * dim:3 * dim]
         gram = (dot(q[:, 0:256], k[:, 0:256], 0, 0), dot(q[:, 128:384], k[:, 128:384], 0, 0))
         qf = q.astype(F32)
         kf = k.astype(F32)
@@ -183,48 +194,35 @@
         ssk = jnp.sum(kf * kf, axis=0, keepdims=True)
         for h in range(heads):
             s = (h * hd) % LANES
-            g_send[b, h, 0:half, :] = pack(head_block(gram, h), s)
             qk = jnp.concatenate([head_row(ssq, h), head_row(ssk, h), jnp.zeros((6, LANES), F32)], axis=0)
-            g_send[b, h, half:G_ROWS, :] = roll(qk, -s)
-
-        @pl.when(b == 0)
-        def _():
-            pl.semaphore_wait(barrier, n - 1)
-
+            g_send[b, h] = pack(head_block(gram, h), s) + beside(qk, s)
+
+    def send_g(b):
         for off in range(1, n):
             g_copy(b, off).start()
-        return carry
-
-    def phase_p(b, carry):
-        rs = rows(b)
-
-        @pl.when(b == 0)
-        def _():
-            load_wout.wait()
-
-        load_dy(b).wait()
-        do = dot(dy_v[rs, :], wout_v[...], 1, 1).astype(BF16)
-        do_v[rs, :] = do
-        v = qkv_v[rs, 2 * dim:3 * dim]
+
+    def grad_o(b):
+        rs = rows(b)
+        do_v[rs, :] = dot(dy_v[rs, :], wout_v[...], 1, 1).astype(BF16)
+
+    def prob_part(b):
+        rs = rows(b)
+        do = do_v[rs, :]
+        v = qkv_v[rs, 0:dim]
         dprob = (dot(do[:, 0:256], v[:, 0:256], 0, 0), dot(do[:, 128:384], v[:, 128:384], 0, 0))
         for h in range(heads):
             p_send[b, h] = pack(head_block(dprob, h), (h * hd) % LANES)
+
+    def send_p(b):
         for off in range(1, n):
             p_copy(b, off).start()
-        return carry
-
-    with scope("phase_g"):
-        lax.fori_loop(0, images, phase_g, 0)
-    with scope("phase_p"):
-        lax.fori_loop(0, images, phase_p, 0)
-
-    load_tau.wait()
-    tau = tau_v[me]
+
     eye = lane == row
     live = lane < hd
     live1 = live[0:1, :]
 
     def owner_a(b):
+        tau = tau_v[me]
         with scope("wait_g"):
             for off in range(1, n):
                 g_copy(b, off).wait_recv()
@@ -232,15 +230,19 @@
         for off in range(1, n):
             total = total + g_recv[b, off - 1]
         gram = unpack(total[0:half, :])
-        ssq = total[half:half + 1, :]
-        ssk = total[half + 1:half + 2, :]
+        sums = jnp.zeros((8, LANES), F32)
+        for i in range(3):
+            mine = (lane[0:8, :] >= 16 * i) & (lane[0:8, :] < 16 * i + 16)
+            sums = jnp.where(mine, roll(total[8 * i:8 * i + 8, :], 16 * i - hd), sums)
+        ssq = sums[0:1, :]
+        ssk = sums[1:2, :]
         rq_col = jnp.sum(jnp.where(eye, lax.rsqrt(ssq), 0.0), axis=1, keepdims=True)
         scale = jnp.where(live, tau * rq_col * lax.rsqrt(ssk), 0.0)
         logits = jnp.where(live, gram * scale, 0.0)
         top = jnp.max(jnp.where(live, logits, -jnp.inf), axis=1, keepdims=True)
         e = jnp.where(live, jnp.exp(logits - top), 0.0)
         p = e / jnp.sum(e, axis=1, keepdims=True)
-        back_a[b, me] = jnp.concatenate([pack(p, 0), jnp.zeros((BACK_ROWS - half, LANES), F32)], axis=0).astype(BF16)
+        back_a[b, me] = pack(p, 0).astype(BF16)
         for off in range(1, n):
             a_copy(b, off).start()
         return p, logits, scale, ssq, ssk
@@ -260,8 +262,8 @@
         cq = -jnp.sum(jnp.where(eye, w_row, 0.0), axis=0, keepdims=True)
         cq = jnp.where(live1, cq / ssq, 0.0)
         ck = jnp.where(live1, -jnp.sum(weighted, axis=0, keepdims=True) / ssk, 0.0)
-        c_row = jnp.broadcast_to(cq + roll(ck, 64), (BACK_ROWS - half, LANES))
-        back_g[b, me] = jnp.concatenate([pack(glog * scale, 0), c_row], axis=0).astype(BF16)
+        c_rows = jnp.concatenate([cq, ck, jnp.zeros((6, LANES), F32)], axis=0)
+        back_g[b, me] = (pack(glog * scale, 0) + beside(c_rows, 0)).astype(BF16)
         for off in range(1, n):
             d_copy(b, off).start()
         return jnp.sum(w_row, axis=0, keepdims=True)
@@ -270,20 +272,21 @@
         with scope(name):
             for off in range(1, n):
                 arrival(b, off).wait_recv()
-        tails = []
+        found_rows = [jnp.zeros((8, LANES), F32) for _ in range(tiles)]
         for h in range(heads):
             got = got_of[b, h].astype(F32)
             which, first, found = pieces(h)
             s = first % LANES
-            low = roll(got[0:half, :], s)
-            high = roll(got[0:half, :], s + 64)
-            val = jnp.concatenate([low, high], axis=0)
+            val = jnp.concatenate([roll(got, s), roll(got, s + 64)], axis=0)
             cols = [jnp.zeros((hd, LANES), F32) for _ in range(2)]
             for t, lo, hi in found:
                 cols[t] = jnp.where((lane >= lo) & (lane < hi), val, 0.0)
             bd[b, which, first:first + hd, :] = jnp.concatenate(cols, axis=1).astype(BF16)
-            tails.append(got[half:half + 1, :])
-        return tails
+            for i in range(3):
+                t, lo = divmod(h * hd + 16 * i, LANES)
+                mine = (lane[0:8, :] >= lo) & (lane[0:8, :] < lo + 16)
+                found_rows[t] = jnp.where(mine, roll(got[8 * i:8 * i + 8, :], lo - hd), found_rows[t])
+        return found_rows
 
     def clear(bd):
         for b in range(images):
@@ -294,17 +297,7 @@
         build(b, back_a, a_arrival, bd_a, "wait_a")
 
     def build_g(b):
-        tails = build(b, back_g, d_arrival, bd_g, "wait_d")
-        for dst, shift in ((cq_v, 0), (ck_v, 64)):
-            vec = [jnp.zeros((1, LANES), F32) for _ in range(tiles)]
-            for h in range(heads):
-                val = roll(tails[h], shift + h * hd)
-                for t in range(tiles):
-                    lo, hi = max(h * hd, t * LANES), min((h + 1) * hd, (t + 1) * LANES)
-                    if lo < hi:
-                        mask = (lane[0:1, :] >= lo - t * LANES) & (lane[0:1, :] < hi - t * LANES)
-                        vec[t] = vec[t] + jnp.where(mask, val, 0.0)
-            dst[b] = jnp.broadcast_to(jnp.concatenate(vec, axis=1), (8, dim))
+        c_v[b] = jnp.concatenate(build(b, back_g, d_arrival, bd_g, "wait_d"), axis=1)
 
     def per_head(tok, mats, transposed):
         c = 1 if transposed else 0
@@ -312,30 +305,45 @@
         right = dot(tok[:, 128:384], mats[1], 1, c)
         return jnp.concatenate([left[:, 0:128], left[:, 128:256] + right[:, 0:128], right[:, 128:256]], axis=1)
 
+    def cols(c):
+        return pl.ds(STARTS[c], STARTS[c + 1] - STARTS[c])
+
     def pair_copy(c):
         return pltpu.make_async_remote_copy(
-            src_ref=part.at[c, :, :, 1 - core], dst_ref=pair_recv.at[c],
+            src_ref=part.at[:, :, 1 - core, :, :, cols(c)], dst_ref=pair_recv.at[:, :, :, :, cols(c)],
             send_sem=pair_ssem.at[c], recv_sem=pair_rsem.at[c],
             device_id=dev(partner), device_id_type=MESH)
 
     def stage_copies(c, stage):
         if stage == 0:
-            refs = ((chip_sum.at[c, :, 1 - px, 0], x_recv.at[c], dev_x),
-                    (chip_sum.at[c, 1 - py, :, 1], y_recv.at[c], dev_y))
+            refs = ((chip_sum.at[:, 1 - px, 0, :, cols(c)], x_recv.at[:, :, cols(c)], dev_x),
+                    (chip_sum.at[1 - py, :, 1, :, cols(c)], y_recv.at[:, :, cols(c)], dev_y))
         else:
-            refs = ((x_send2.at[c], x_recv2.at[c], dev_x), (y_send2.at[c], y_recv2.at[c], dev_y))
+            refs = ((x_send2.at[:, cols(c)], x_recv2.at[:, cols(c)], dev_x),
+                    (y_send2.at[:, cols(c)], y_recv2.at[:, cols(c)], dev_y))
         return [pltpu.make_async_remote_copy(
             src_ref=src, dst_ref=dst, send_sem=st_ssem.at[c, stage, i], recv_sem=st_rsem.at[c, stage, i],
             device_id=dev(d), device_id_type=MESH) for i, (src, dst, d) in enumerate(refs)]
 
-    def rs0(c, value):
-        part[c] = value.reshape(2, 2, 2, 2, half, dim)
+    def weight_part(b, col, lhs, rhs, contract):
+        value = dot(lhs, rhs, contract, 0).reshape(2, 2, 2, 2, half, dim)
+        if b:
+            value = value + part[:, :, :, :, :, col:col + dim]
+        part[:, :, :, :, :, col:col + dim] = value
+
+    def part_o(b):
+        weight_part(b, 0, o_v[rows(b), :], dy_v[rows(b), :], 0)
+
+    def part_qkv(b, i):
+        weight_part(b, (1 + i) * dim, ut_v[:, b * tokens:(b + 1) * tokens], dqkv_v[rows(b), i * dim:(i + 1) * dim], 1)
+
+    def rs0(c):
         pair_copy(c).start()
 
     def rs1(c):
         with scope("wait_pair"):
             pair_copy(c).wait_recv()
-        chip_sum[c] = part[c, :, :, core] + pair_recv[c]
+        chip_sum[:, :, :, :, cols(c)] = part[:, :, core, :, :, cols(c)] + pair_recv[:, :, :, :, cols(c)]
         for copy in stage_copies(c, 0):
             copy.start()
 
@@ -343,38 +351,38 @@
         with scope("wait_st0"):
             for copy in stage_copies(c, 0):
                 copy.wait_recv()
-        x_send2[c] = chip_sum[c, py, 1 - px, 1] + y_recv[c, 1 - px]
-        y_send2[c] = chip_sum[c, 1 - py, px, 0] + x_recv[c, 1 - py]
+        x_send2[:, cols(c)] = chip_sum[py, 1 - px, 1, :, cols(c)] + y_recv[1 - px, :, cols(c)]
+        y_send2[:, cols(c)] = chip_sum[1 - py, px, 0, :, cols(c)] + x_recv[1 - py, :, cols(c)]
         for copy in stage_copies(c, 1):
             copy.start()
 
     def rs3(c):
-        own_a = chip_sum[c, py, px, 0] + x_recv[c, py]
-        own_b = chip_sum[c, py, px, 1] + y_recv[c, px]
+        own_a = chip_sum[py, px, 0, :, cols(c)] + x_recv[py, :, cols(c)]
+        own_b = chip_sum[py, px, 1, :, cols(c)] + y_recv[px, :, cols(c)]
         with scope("wait_st1"):
             for copy in stage_copies(c, 1):
                 copy.wait_recv()
-        return jnp.concatenate([own_a + y_recv2[c], own_b + x_recv2[c]], axis=0).astype(BF16)
+        return jnp.concatenate([own_a + y_recv2[:, cols(c)], own_b + x_recv2[:, cols(c)]], axis=0).astype(BF16)
 
     def heads_out(b):
         rs = rows(b)
-        o_v[rs, :] = per_head(qkv_v[rs, 2 * dim:3 * dim], bd_a[b], True).astype(BF16)
+        o_v[rs, :] = per_head(qkv_v[rs, 0:dim], bd_a[b], True).astype(BF16)
 
     def grad_v(b):
         rs = rows(b)
-        dqkv_v[rs, 2 * dim:3 * dim] = per_head(do_v[rs, :], bd_a[b], False).astype(BF16)
+        dqkv_v[rs, 0:dim] = per_head(do_v[rs, :], bd_a[b], False).astype(BF16)
 
     def grad_q(b):
         rs = rows(b)
-        q = qkv_v[rs, 0:dim]
-        k = qkv_v[rs, dim:2 * dim]
-        dqkv_v[rs, 0:dim] = (per_head(k, bd_g[b], True) + cq_v[b, 0:1, :] * q.astype(F32)).astype(BF16)
+        q = qkv_v[rs, dim:2 * dim]
+        k = qkv_v[rs, 2 * dim:3 * dim]
+        dqkv_v[rs, dim:2 * dim] = (per_head(k, bd_g[b], True) + c_v[b, 0:1, :] * q.astype(F32)).astype(BF16)
 
     def grad_k(b):
         rs = rows(b)
-        q = qkv_v[rs, 0:dim]
-        k = qkv_v[rs, dim:2 * dim]
-        dqkv_v[rs, dim:2 * dim] = (per_head(q, bd_g[b], False) + ck_v[b, 0:1, :] * k.astype(F32)).astype(BF16)
+        q = qkv_v[rs, dim:2 * dim]
+        k = qkv_v[rs, 2 * dim:3 * dim]
+        dqkv_v[rs, 2 * dim:3 * dim] = (per_head(q, bd_g[b], False) + c_v[b, 1:2, :] * k.astype(F32)).astype(BF16)
 
     def out_y(b):
         rs = rows(b)
@@ -396,58 +404,103 @@
         mx = jnp.mean(a * xhat, axis=-1, keepdims=True)
         dx_v[rs, :] = (dy_v[rs, :].astype(F32) + rstd_v[rs, :] * (a - ma - xhat * mx)).astype(BF16)
 
-    clear(bd_a)
-    clear(bd_g)
+    with scope("phase_1"):
+        clear(bd_a)
+        clear(bd_g)
+        load_x(0).wait()
+        load_gain.wait()
+        load_bias.wait()
+        layer_norm(0)
+        load_w[1].wait()
+        load_w[2].wait()
+        load_x(1).wait()
+        project_qk(0)
+        layer_norm(1)
+        gram_part(0)
+    with scope("wait_barrier"):
+        pl.semaphore_wait(barrier, n - 1)
+    with scope("phase_2"):
+        send_g(0)
+        project_qk(1)
+        gram_part(1)
+        send_g(1)
+    with scope("phase_3"):
+        load_wout.wait()
+        load_dy(0).wait()
+        load_w[0].wait()
+        load_dy(1).wait()
+        load_tau.wait()
+        project_v(0)
+        grad_o(0)
+        prob_part(0)
+        send_p(0)
+        grad_o(1)
+        project_v(1)
     with scope("owner_a0"):
         state0 = owner_a(0)
+    with scope("phase_4"):
+        prob_part(1)
+        send_p(1)
     with scope("owner_a1"):
         state1 = owner_a(1)
+    with scope("transpose"):
+        for b in range(images):
+            ut_v[:, b * tokens:(b + 1) * tokens] = u_v[rows(b), :].T
     with scope("owner_g0"):
         w0 = owner_g(0, state0)
     build_a(0)
-    with scope("heads_out"):
+    with scope("group1"):
         heads_out(0)
-    with scope("grad_v"):
         grad_v(0)
+        part_o(0)
     with scope("owner_g1"):
         w1 = owner_g(1, state1)
     build_a(1)
-    with scope("heads_out"):
+    with scope("group2"):
         heads_out(1)
-    with scope("part0"):
-        rs0(0, dot(o_v[...], dy_v[...], 0, 0))
-    with scope("grad_v"):
+        part_o(1)
+        rs0(0)
+    with scope("group3"):
+        part_qkv(0, 0)
         grad_v(1)
-    with scope("part1"):
-        rs0(1, dot(u_v[...], dqkv_v[:, 2 * dim:3 * dim], 0, 0))
     rs1(0)
+    with scope("group3b"):
+        part_qkv(1, 0)
+        rs0(1)
     build_g(0)
-    with scope("grad_q"):
+    with scope("group4"):
         grad_q(0)
+        part_qkv(0, 1)
     build_g(1)
-    with scope("grad_q"):
+    rs1(1)
+    with scope("group5"):
         grad_q(1)
-    rs1(1)
-    with scope("part2"):
-        rs0(2, dot(u_v[...], dqkv_v[:, 0:dim], 0, 0))
-    with scope("grad_k"):
+        part_qkv(1, 1)
+        rs0(2)
         grad_k(0)
-    with scope("grad_k"):
         grad_k(1)
+        part_qkv(0, 2)
     rs1(2)
-    with scope("part3"):
-        rs0(3, dot(u_v[...], dqkv_v[:, dim:2 * dim], 0, 0))
+    with scope("group6"):
+        part_qkv(1, 2)
+        rs0(3)
+        rs0(4)
     rs2(0)
-    with scope("grad_u"):
+    with scope("out_y"):
+        out_y(0)
+        out_y(1)
+    rs1(3)
+    rs1(4)
+    rs2(1)
+    with scope("group7"):
         sg0, sb0 = grad_u(0)
-    rs1(3)
-    rs2(1)
-    with scope("grad_u"):
+    rs2(2)
+    with scope("group8"):
         sg1, sb1 = grad_u(1)
 
     sg = sg0 + sg1
     sb = sb0 + sb1
-    st = jnp.where(lane[0:1, :] == me, (w0 + w1) / tau, 0.0)
+    st = jnp.where(lane[0:1, :] == me, (w0 + w1) / tau_v[me], 0.0)
     ln_rows = [val[:, t * LANES:(t + 1) * LANES] for val in (sg, sb) for t in range(tiles)]
     ln_all[me] = jnp.concatenate(ln_rows + [st, jnp.zeros((1, LANES), F32)], axis=0)
 
@@ -460,20 +513,16 @@
     for off in range(1, n):
         ln_copy(off, me).start()
 
-    rs2(2)
-    with scope("out_dx"):
+    rs2(3)
+    rs2(4)
+    with scope("group9"):
         out_dx(0)
-    with scope("out_y"):
-        out_y(0)
-    rs2(3)
-    with scope("out_dx"):
         out_dx(1)
-    with scope("out_y"):
-        out_y(1)
     gwout_ref[...] = rs3(0)
     gwqkv_ref[:, 2 * dim:3 * dim] = rs3(1)
     gwqkv_ref[:, 0:dim] = rs3(2)
-    gwqkv_ref[:, dim:2 * dim] = rs3(3)
+    gwqkv_ref[:, dim:dim + 256] = rs3(3)
+    gwqkv_ref[:, dim + 256:2 * dim] = rs3(4)
     with scope("wait_ln"):
         for off in range(1, n):
             ln_copy(off, lax.rem(me + n - off, n)).wait_recv()
@@ -489,7 +538,7 @@
                 p_copy(b, off).wait_send()
                 a_copy(b, off).wait_send()
                 d_copy(b, off).wait_send()
-        for c in range(4):
+        for c in range(5):
             pair_copy(c).wait_send()
             for stage in range(2):
                 for copy in stage_copies(c, stage):
@@ -499,16 +548,20 @@
 
 
 def finish(dim, heads, y_v, dx_v, gwqkv_v, gwout_v, sums_v,
-           y_hbm, dx_hbm, gwqkv_hbm, gwout_hbm, ggain_ref, gbias_ref, gtau_ref, sem):
-    pairs = ((y_v, y_hbm), (dx_v, dx_hbm), (gwqkv_v, gwqkv_hbm), (gwout_v, gwout_hbm))
+           y_hbm, dx_hbm, gwqkv_hbm, gwout_hbm, ggain_hbm, gbias_hbm, gtau_hbm,
+           gain_v, bias_v, tau_v, sem):
+    tiles = dim // LANES
+    pairs = ((y_v, y_hbm), (dx_v, dx_hbm), (gwqkv_v, gwqkv_hbm), (gwout_v, gwout_hbm),
+             (gain_v, ggain_hbm), (bias_v, gbias_hbm), (tau_v, gtau_hbm))
     copies = [pltpu.make_async_copy(src, dst, sem.at[i]) for i, (src, dst) in enumerate(pairs)]
-    for copy in copies:
+    for copy in copies[:4]:
         copy.start()
-    tiles = dim // LANES
     for t in range(tiles):
-        ggain_ref[t * LANES:(t + 1) * LANES] = sums_v[t, :]
-        gbias_ref[t * LANES:(t + 1) * LANES] = sums_v[tiles + t, :]
-    gtau_ref[...] = sums_v[2 * tiles, 0:heads]
+        gain_v[t * LANES:(t + 1) * LANES] = sums_v[t, :]
+        bias_v[t * LANES:(t + 1) * LANES] = sums_v[tiles + t, :]
+    tau_v[...] = sums_v[2 * tiles, 0:heads]
+    for copy in copies[4:]:
+        copy.start()
     for copy in copies:
         copy.wait()
 
@@ -549,6 +602,7 @@
                 pltpu.VMEM((num, 1), F32),
                 pltpu.VMEM((num, dim), BF16),
                 pltpu.VMEM((num, dim), BF16),
+                pltpu.VMEM((dim, num), BF16),
                 pltpu.VMEM((num, 3 * dim), BF16),
                 pltpu.VMEM((num, dim), BF16),
                 pltpu.VMEM((num, dim), BF16),
@@ -562,24 +616,23 @@
                 pltpu.VMEM((images, 2, 256, 256), BF16),
                 pltpu.VMEM((images, 2, 256, 256), BF16),
                 pltpu.VMEM((images, 8, dim), F32),
-                pltpu.VMEM((images, 8, dim), F32),
-                pltpu.VMEM((4, 2, 2, 2, 2, half, dim), F32),
-                pltpu.VMEM((4, 2, 2, 2, half, dim), F32),
-                pltpu.VMEM((4, 2, 2, 2, half, dim), F32),
-                pltpu.VMEM((4, 2, half, dim), F32),
-                pltpu.VMEM((4, 2, half, dim), F32),
-                pltpu.VMEM((4, half, dim), F32),
-                pltpu.VMEM((4, half, dim), F32),
-                pltpu.VMEM((4, half, dim), F32),
-                pltpu.VMEM((4, half, dim), F32),
+                pltpu.VMEM((2, 2, 2, 2, half, 4 * dim), F32),
+                pltpu.VMEM((2, 2, 2, half, 4 * dim), F32),
+                pltpu.VMEM((2, 2, 2, half, 4 * dim), F32),
+                pltpu.VMEM((2, half, 4 * dim), F32),
+                pltpu.VMEM((2, half, 4 * dim), F32),
+                pltpu.VMEM((half, 4 * dim), F32),
+                pltpu.VMEM((half, 4 * dim), F32),
+                pltpu.VMEM((half, 4 * dim), F32),
+                pltpu.VMEM((half, 4 * dim), F32),
                 pltpu.VMEM((n, 8, LANES), F32),
-                dma((2 * images + 5,)),
+                dma((2 * images + 8,)),
                 dma((images, n - 1)), dma((images, n - 1)),
                 dma((images, n - 1)), dma((images, n - 1)),
                 dma((images, n - 1)), dma((images, n - 1)),
                 dma((images, n - 1)), dma((images, n - 1)),
-                dma((4,)), dma((4,)),
-                dma((4, 2, 2)), dma((4, 2, 2)),
+                dma((5,)), dma((5,)),
+                dma((5, 2, 2)), dma((5, 2, 2)),
                 dma((n - 1,)), dma((n - 1,)),
             ],
             compiler_params=params,
@@ -597,8 +650,8 @@
                 jax.ShapeDtypeStruct((heads,), F32),
             ),
             in_specs=[vmem] * 5,
-            out_specs=(hbm, hbm, hbm, hbm, vmem, vmem, vmem),
-            scratch_shapes=[dma((4,))],
+            out_specs=(hbm,) * 7,
+            scratch_shapes=[pltpu.VMEM((dim,), F32), pltpu.VMEM((dim,), F32), pltpu.VMEM((heads,), F32), dma((7,))],
             compiler_params=pltpu.CompilerParams(vmem_limit_bytes=2**20),
             name="xca_finish",
         )(y, dx, gwqkv, gwout, sums)

time: 37.5 us -> 35.2 us (0.939)
  Pallas kernels: 36.6 us -> 34.3 us
    pallas_call x1, Pallas kernels: 34.3 us -> 32.6 us  [local_step(): pl.pallas_call(functools.partial(body, images, tokens, dim, heads, n), ou...]
    pallas_call x1, Pallas kernels: 2.29 us -> 1.76 us  [local_step(): pl.pallas_call(functools.partial(finish, dim, heads), out_shape=(jax.Shap...]
where the time goes in v1:
time: 35.2 us; the launch traced here: 35.1 us
  Pallas kernels  34.3 us (97%)
  between operations  0.8 us (2%)
    pallas_call x1, Pallas kernels, local_step(): pl.pallas_call(functools.partial(body, images, tokens, dim, heads, n), ou...  32.6 us
    pallas_call x1, Pallas kernels, local_step(): pl.pallas_call(functools.partial(finish, dim, heads), out_shape=(jax.Shap...  1.76 us

profile of v1, /device:TPU:0, one launch (start us, length us, event | category | flops | bytes accessed | tf_op | source)
XLA Modules:
  0.0 35.1 jit_solution(15697578572558875184)
XLA Ops:
  0.6 32.6 %xca_step.1 = (bf16[2048,384]{1,0:T(8,128)(2,1)S(1)}, bf16[2048,384]{1,0:T(8,128)(2,1)S(1)}, bf16[48,1152]{1,0:T(8,128)(2,1)S(1)}, bf16[48,384]{1,0:T(8,128)(2,1)S(1)}, f32[8,128]{1,0:T(8,128)S(1)}) custom-call(bf16[2,1024,384]{2,1,0:T(8,128)(2,1)} %x_hbm.1, bf16[2,1024,384]{2,1,0:T(8,128)(2,1)} %dy_hbm.1, f32[384]{0:T(512)} %gain_hbm.1, f32[384]{0:T(512)} %bias_hbm.1, ...), custom_call_target="tpu_custom_call" | custom-call | tf_op jit(solution)/shard_map/xca_step/pallas_call | solution.py:582
  33.2 1.8 %xca_finish.1 = (bf16[2048,384]{1,0:T(8,128)(2,1)}, bf16[2048,384]{1,0:T(8,128)(2,1)}, bf16[48,1152]{1,0:T(8,128)(2,1)}, bf16[48,384]{1,0:T(8,128)(2,1)}, f32[384]{0:T(512)}, /*index=5*/f32[384]{0:T(512)}, f32[8]{0:T(128)}) custom-call(bf16[2048,384]{1,0:T(8,128)(2,1)S(1)} %get-tuple-element.19.y_v, bf16[2048,384]{1,0:T(8,128)(2,1)S(1)} %get-tuple-element.20.dx_v, ...), custom_call_target="tpu_custom_call" | custom-call | tf_op jit(solution)/shard_map/xca_finish/pallas_call | solution.py:641

commit v2 on v1

--- a/solution.py
+++ b/solution.py
@@ -17,6 +17,8 @@
 P_ROWS = 24
 BACK_ROWS = 24
 STARTS = (0, 384, 768, 1152, 1408, 1536)
+FAR, NEAR, PASSED = 0, 1, 2
+LATE = 3
 SPLIT = 3
 
 
@@ -40,7 +42,7 @@
          g_send, g_recv, p_send, p_recv, back_a, back_g, bd_a, bd_g, c_v,
          part, pair_recv, chip_sum, x_recv, y_recv, x_send2, y_send2, x_recv2, y_recv2, ln_all,
          load_sem, g_ssem, g_rsem, p_ssem, p_rsem, a_ssem, a_rsem, d_ssem, d_rsem,
-         pair_ssem, pair_rsem, st_ssem, st_rsem, ln_ssem, ln_rsem):
+         pair_ssem, pair_rsem, st_ssem, far_rsem, near_rsem, passed_rsem, ln_ssem, ln_rsem):
     hd = dim // heads
     half = hd // 2
     tiles = dim // LANES
@@ -63,21 +65,20 @@
         return pltpu.make_async_copy(x_hbm.at[b], x_v.at[rows(b)], load_sem.at[b])
 
     def load_dy(b):
-        return pltpu.make_async_copy(dy_hbm.at[b], dy_v.at[rows(b)], load_sem.at[images + b])
-
-    load_w = [pltpu.make_async_copy(wqkv_hbm.at[:, pl.ds((i + 2) % 3 * dim, dim)], wqkv_v.at[:, pl.ds(i * dim, dim)],
-                                    load_sem.at[2 * images + 5 + i]) for i in range(3)]
-    load_wout = pltpu.make_async_copy(wout_hbm, wout_v, load_sem.at[2 * images])
-    load_gain = pltpu.make_async_copy(gain_hbm, gain_v, load_sem.at[2 * images + 2])
-    load_bias = pltpu.make_async_copy(bias_hbm, bias_v, load_sem.at[2 * images + 3])
-    load_tau = pltpu.make_async_copy(tau_hbm, tau_v, load_sem.at[2 * images + 4])
+        return pltpu.make_async_copy(dy_hbm.at[b], dy_v.at[rows(b)], load_sem.at[images])
+
+    load_v = pltpu.make_async_copy(wqkv_hbm.at[:, pl.ds(2 * dim, dim)], wqkv_v.at[:, pl.ds(0, dim)], load_sem.at[images + 1])
+    load_qk = pltpu.make_async_copy(wqkv_hbm.at[:, pl.ds(0, 2 * dim)], wqkv_v.at[:, pl.ds(dim, 2 * dim)], load_sem.at[images + 2])
+    load_wout = pltpu.make_async_copy(wout_hbm, wout_v, load_sem.at[images + 3])
+    load_gain = pltpu.make_async_copy(gain_hbm, gain_v, load_sem.at[images + 4])
+    load_bias = pltpu.make_async_copy(bias_hbm, bias_v, load_sem.at[images + 5])
+    load_tau = pltpu.make_async_copy(tau_hbm, tau_v, load_sem.at[images + 6])
     load_x(0).start()
     load_gain.start()
     load_bias.start()
-    load_w[1].start()
-    load_w[2].start()
+    load_qk.start()
     load_x(1).start()
-    load_w[0].start()
+    load_v.start()
     load_wout.start()
     load_dy(0).start()
     load_dy(1).start()
@@ -130,12 +131,15 @@
     def beside(val, s):
         return jnp.concatenate([jnp.where(side, roll(val, hd - 16 * i - s), 0.0) for i in range(3)], axis=0)
 
+    def all_of(ref, ssem, rsem):
+        return pltpu.make_async_remote_copy(
+            src_ref=ref, dst_ref=ref, send_sem=ssem, recv_sem=rsem, device_id=dev(partner), device_id_type=MESH)
+
     def exchange(send, recv, ssem, rsem, b, off):
         dst = lax.rem(me + off, n)
         return pltpu.make_async_remote_copy(
             src_ref=send.at[b, dst], dst_ref=recv.at[b, off - 1],
-            send_sem=ssem.at[b, off - 1], recv_sem=rsem.at[b, off - 1],
-            device_id=dev(dst), device_id_type=MESH)
+            send_sem=ssem, recv_sem=rsem.at[b], device_id=dev(dst), device_id_type=MESH)
 
     def g_copy(b, off):
         return exchange(g_send, g_recv, g_ssem, g_rsem, b, off)
@@ -143,23 +147,16 @@
     def p_copy(b, off):
         return exchange(p_send, p_recv, p_ssem, p_rsem, b, off)
 
-    def spread(buf, ssem, rsem, b, off, src):
+    def spread(buf, ssem, rsem, b, off):
         return pltpu.make_async_remote_copy(
-            src_ref=buf.at[b, src], dst_ref=buf.at[b, src],
-            send_sem=ssem.at[b, off - 1], recv_sem=rsem.at[b, off - 1],
+            src_ref=buf.at[b, me], dst_ref=buf.at[b, me], send_sem=ssem, recv_sem=rsem.at[b],
             device_id=dev(lax.rem(me + off, n)), device_id_type=MESH)
 
     def a_copy(b, off):
-        return spread(back_a, a_ssem, a_rsem, b, off, me)
-
-    def a_arrival(b, off):
-        return spread(back_a, a_ssem, a_rsem, b, off, lax.rem(me + n - off, n))
+        return spread(back_a, a_ssem, a_rsem, b, off)
 
     def d_copy(b, off):
-        return spread(back_g, d_ssem, d_rsem, b, off, me)
-
-    def d_arrival(b, off):
-        return spread(back_g, d_ssem, d_rsem, b, off, lax.rem(me + n - off, n))
+        return spread(back_g, d_ssem, d_rsem, b, off)
 
     def layer_norm(b):
         rs = rows(b)
@@ -224,8 +221,7 @@
     def owner_a(b):
         tau = tau_v[me]
         with scope("wait_g"):
-            for off in range(1, n):
-                g_copy(b, off).wait_recv()
+            all_of(g_recv.at[b], g_ssem, g_rsem.at[b]).wait_recv()
         total = g_send[b, me]
         for off in range(1, n):
             total = total + g_recv[b, off - 1]
@@ -250,8 +246,7 @@
     def owner_g(b, state):
         p, logits, scale, ssq, ssk = state
         with scope("wait_p"):
-            for off in range(1, n):
-                p_copy(b, off).wait_recv()
+            all_of(p_recv.at[b], p_ssem, p_rsem.at[b]).wait_recv()
         total = p_send[b, me]
         for off in range(1, n):
             total = total + p_recv[b, off - 1]
@@ -268,10 +263,9 @@
             d_copy(b, off).start()
         return jnp.sum(w_row, axis=0, keepdims=True)
 
-    def build(b, got_of, arrival, bd, name):
+    def build(b, got_of, ssem, rsem, bd, name):
         with scope(name):
-            for off in range(1, n):
-                arrival(b, off).wait_recv()
+            all_of(got_of.at[b, pl.ds(0, n - 1)], ssem, rsem.at[b]).wait_recv()
         found_rows = [jnp.zeros((8, LANES), F32) for _ in range(tiles)]
         for h in range(heads):
             got = got_of[b, h].astype(F32)
@@ -294,10 +288,10 @@
             bd[b, 1, 0:SPLIT * hd - LANES, :] = jnp.zeros((SPLIT * hd - LANES, 256), BF16)
 
     def build_a(b):
-        build(b, back_a, a_arrival, bd_a, "wait_a")
+        build(b, back_a, a_ssem, a_rsem, bd_a, "wait_a")
 
     def build_g(b):
-        c_v[b] = jnp.concatenate(build(b, back_g, d_arrival, bd_g, "wait_d"), axis=1)
+        c_v[b] = jnp.concatenate(build(b, back_g, d_ssem, d_rsem, bd_g, "wait_d"), axis=1)
 
     def per_head(tok, mats, transposed):
         c = 1 if transposed else 0
@@ -311,19 +305,27 @@
     def pair_copy(c):
         return pltpu.make_async_remote_copy(
             src_ref=part.at[:, :, 1 - core, :, :, cols(c)], dst_ref=pair_recv.at[:, :, :, :, cols(c)],
-            send_sem=pair_ssem.at[c], recv_sem=pair_rsem.at[c],
+            send_sem=pair_ssem, recv_sem=pair_rsem.at[c],
             device_id=dev(partner), device_id_type=MESH)
 
+    def arrival_sem(c, stage):
+        if stage == FAR:
+            return far_rsem.at[c]
+        return near_rsem if stage == NEAR else passed_rsem.at[0 if c < LATE else 1]
+
     def stage_copies(c, stage):
-        if stage == 0:
-            refs = ((chip_sum.at[:, 1 - px, 0, :, cols(c)], x_recv.at[:, :, cols(c)], dev_x),
-                    (chip_sum.at[1 - py, :, 1, :, cols(c)], y_recv.at[:, :, cols(c)], dev_y))
+        if stage == FAR:
+            refs = ((chip_sum.at[1 - py, 1 - px, 0, :, cols(c)], x_recv.at[1 - py, :, cols(c)], dev_x),
+                    (chip_sum.at[1 - py, 1 - px, 1, :, cols(c)], y_recv.at[1 - px, :, cols(c)], dev_y))
+        elif stage == NEAR:
+            refs = ((chip_sum.at[py, 1 - px, 0, :, cols(c)], x_recv.at[py, :, cols(c)], dev_x),
+                    (chip_sum.at[1 - py, px, 1, :, cols(c)], y_recv.at[px, :, cols(c)], dev_y))
         else:
             refs = ((x_send2.at[:, cols(c)], x_recv2.at[:, cols(c)], dev_x),
                     (y_send2.at[:, cols(c)], y_recv2.at[:, cols(c)], dev_y))
         return [pltpu.make_async_remote_copy(
-            src_ref=src, dst_ref=dst, send_sem=st_ssem.at[c, stage, i], recv_sem=st_rsem.at[c, stage, i],
-            device_id=dev(d), device_id_type=MESH) for i, (src, dst, d) in enumerate(refs)]
+            src_ref=src, dst_ref=dst, send_sem=st_ssem.at[stage], recv_sem=arrival_sem(c, stage),
+            device_id=dev(d), device_id_type=MESH) for src, dst, d in refs]
 
     def weight_part(b, col, lhs, rhs, contract):
         value = dot(lhs, rhs, contract, 0).reshape(2, 2, 2, 2, half, dim)
@@ -344,25 +346,22 @@
         with scope("wait_pair"):
             pair_copy(c).wait_recv()
         chip_sum[:, :, :, :, cols(c)] = part[:, :, core, :, :, cols(c)] + pair_recv[:, :, :, :, cols(c)]
-        for copy in stage_copies(c, 0):
-            copy.start()
+        for stage in (FAR, NEAR):
+            for copy in stage_copies(c, stage):
+                copy.start()
 
     def rs2(c):
         with scope("wait_st0"):
-            for copy in stage_copies(c, 0):
-                copy.wait_recv()
+            all_of(x_recv.at[:, :, cols(c)], st_ssem.at[FAR], far_rsem.at[c]).wait_recv()
         x_send2[:, cols(c)] = chip_sum[py, 1 - px, 1, :, cols(c)] + y_recv[1 - px, :, cols(c)]
         y_send2[:, cols(c)] = chip_sum[1 - py, px, 0, :, cols(c)] + x_recv[1 - py, :, cols(c)]
-        for copy in stage_copies(c, 1):
+        for copy in stage_copies(c, PASSED):
             copy.start()
 
-    def rs3(c):
-        own_a = chip_sum[py, px, 0, :, cols(c)] + x_recv[py, :, cols(c)]
-        own_b = chip_sum[py, px, 1, :, cols(c)] + y_recv[px, :, cols(c)]
-        with scope("wait_st1"):
-            for copy in stage_copies(c, 1):
-                copy.wait_recv()
-        return jnp.concatenate([own_a + y_recv2[:, cols(c)], own_b + x_recv2[:, cols(c)]], axis=0).astype(BF16)
+    def rs3(lo, hi):
+        own_a = chip_sum[py, px, 0, :, lo:hi] + x_recv[py, :, lo:hi]
+        own_b = chip_sum[py, px, 1, :, lo:hi] + y_recv[px, :, lo:hi]
+        return jnp.concatenate([own_a + y_recv2[:, lo:hi], own_b + x_recv2[:, lo:hi]], axis=0).astype(BF16)
 
     def heads_out(b):
         rs = rows(b)
@@ -388,8 +387,8 @@
         rs = rows(b)
         y_v[rs, :] = (x_v[rs, :].astype(F32) + dot(o_v[rs, :], wout_v[...], 1, 0)).astype(BF16)
 
-    def grad_u(b):
-        rs = rows(b)
+    def grad_u(b, i):
+        rs = pl.ds(b * tokens + i * (tokens // 2), tokens // 2)
         du = dot(dqkv_v[rs, :], wqkv_v[...], 1, 1).astype(BF16)
         du_v[rs, :] = du
         du = du.astype(F32)
@@ -411,8 +410,7 @@
         load_gain.wait()
         load_bias.wait()
         layer_norm(0)
-        load_w[1].wait()
-        load_w[2].wait()
+        load_qk.wait()
         load_x(1).wait()
         project_qk(0)
         layer_norm(1)
@@ -426,9 +424,8 @@
         send_g(1)
     with scope("phase_3"):
         load_wout.wait()
-        load_dy(0).wait()
-        load_w[0].wait()
-        load_dy(1).wait()
+        pltpu.make_async_copy(dy_v, dy_v, load_sem.at[images]).wait()
+        load_v.wait()
         load_tau.wait()
         project_v(0)
         grad_o(0)
@@ -481,70 +478,72 @@
         grad_k(1)
         part_qkv(0, 2)
     rs1(2)
+    rs2(0)
     with scope("group6"):
         part_qkv(1, 2)
         rs0(3)
         rs0(4)
-    rs2(0)
     with scope("out_y"):
         out_y(0)
         out_y(1)
     rs1(3)
     rs1(4)
     rs2(1)
+    ln_sums = []
     with scope("group7"):
-        sg0, sb0 = grad_u(0)
+        ln_sums.append(grad_u(0, 0))
+        ln_sums.append(grad_u(0, 1))
+        ln_sums.append(grad_u(1, 0))
     rs2(2)
     with scope("group8"):
-        sg1, sb1 = grad_u(1)
-
-    sg = sg0 + sg1
-    sb = sb0 + sb1
+        ln_sums.append(grad_u(1, 1))
+
+    sg = sum(val[0] for val in ln_sums)
+    sb = sum(val[1] for val in ln_sums)
     st = jnp.where(lane[0:1, :] == me, (w0 + w1) / tau_v[me], 0.0)
     ln_rows = [val[:, t * LANES:(t + 1) * LANES] for val in (sg, sb) for t in range(tiles)]
     ln_all[me] = jnp.concatenate(ln_rows + [st, jnp.zeros((1, LANES), F32)], axis=0)
 
-    def ln_copy(off, src):
+    def ln_copy(off):
         return pltpu.make_async_remote_copy(
-            src_ref=ln_all.at[src], dst_ref=ln_all.at[src],
-            send_sem=ln_ssem.at[off - 1], recv_sem=ln_rsem.at[off - 1],
+            src_ref=ln_all.at[me], dst_ref=ln_all.at[me], send_sem=ln_ssem, recv_sem=ln_rsem,
             device_id=dev(lax.rem(me + off, n)), device_id_type=MESH)
 
     for off in range(1, n):
-        ln_copy(off, me).start()
+        ln_copy(off).start()
 
     rs2(3)
     rs2(4)
     with scope("group9"):
         out_dx(0)
         out_dx(1)
-    gwout_ref[...] = rs3(0)
-    gwqkv_ref[:, 2 * dim:3 * dim] = rs3(1)
-    gwqkv_ref[:, 0:dim] = rs3(2)
-    gwqkv_ref[:, dim:dim + 256] = rs3(3)
-    gwqkv_ref[:, dim + 256:2 * dim] = rs3(4)
+    split = STARTS[LATE]
+    with scope("wait_near"):
+        all_of(x_recv, st_ssem.at[NEAR], near_rsem).wait_recv()
+    with scope("wait_st1"):
+        all_of(x_recv.at[:, :, pl.ds(0, split)], st_ssem.at[PASSED], passed_rsem.at[0]).wait_recv()
+    gwout_ref[...] = rs3(0, dim)
+    gwqkv_ref[:, 2 * dim:3 * dim] = rs3(dim, 2 * dim)
+    gwqkv_ref[:, 0:dim] = rs3(2 * dim, 3 * dim)
     with scope("wait_ln"):
-        for off in range(1, n):
-            ln_copy(off, lax.rem(me + n - off, n)).wait_recv()
+        all_of(ln_all.at[pl.ds(0, n - 1)], ln_ssem, ln_rsem).wait_recv()
     sums = ln_all[0]
     for d in range(1, n):
         sums = sums + ln_all[d]
     sums_ref[...] = sums
+    with scope("wait_st1"):
+        all_of(x_recv.at[:, :, pl.ds(split, 4 * dim - split)], st_ssem.at[PASSED], passed_rsem.at[1]).wait_recv()
+    gwqkv_ref[:, dim:2 * dim] = rs3(3 * dim, 4 * dim)
 
     with scope("final"):
-        for b in range(images):
-            for off in range(1, n):
-                g_copy(b, off).wait_send()
-                p_copy(b, off).wait_send()
-                a_copy(b, off).wait_send()
-                d_copy(b, off).wait_send()
-        for c in range(5):
-            pair_copy(c).wait_send()
-            for stage in range(2):
-                for copy in stage_copies(c, stage):
-                    copy.wait_send()
-        for off in range(1, n):
-            ln_copy(off, me).wait_send()
+        all_of(g_recv, g_ssem, g_rsem.at[0]).wait_send()
+        all_of(p_recv, p_ssem, p_rsem.at[0]).wait_send()
+        all_of(back_a.at[:, pl.ds(0, n - 1)], a_ssem, a_rsem.at[0]).wait_send()
+        all_of(back_g.at[:, pl.ds(0, n - 1)], d_ssem, d_rsem.at[0]).wait_send()
+        all_of(pair_recv, pair_ssem, pair_rsem.at[0]).wait_send()
+        for stage in (FAR, NEAR, PASSED):
+            all_of(x_recv, st_ssem.at[stage], near_rsem).wait_send()
+        all_of(ln_all.at[pl.ds(0, n - 1)], ln_ssem, ln_rsem).wait_send()
 
 
 def finish(dim, heads, y_v, dx_v, gwqkv_v, gwout_v, sums_v,
@@ -626,14 +625,14 @@
                 pltpu.VMEM((half, 4 * dim), F32),
                 pltpu.VMEM((half, 4 * dim), F32),
                 pltpu.VMEM((n, 8, LANES), F32),
-                dma((2 * images + 8,)),
-                dma((images, n - 1)), dma((images, n - 1)),
-                dma((images, n - 1)), dma((images, n - 1)),
-                dma((images, n - 1)), dma((images, n - 1)),
-                dma((images, n - 1)), dma((images, n - 1)),
-                dma((5,)), dma((5,)),
-                dma((5, 2, 2)), dma((5, 2, 2)),
-                dma((n - 1,)), dma((n - 1,)),
+                dma((images + 7,)),
+                dma, dma((images,)),
+                dma, dma((images,)),
+                dma, dma((images,)),
+                dma, dma((images,)),
+                dma, dma((5,)),
+                dma((3,)), dma((5,)), dma, dma((2,)),
+                dma, dma,
             ],
             compiler_params=params,
             name="xca_step",

time: 35.2 us -> 33.5 us (0.952)
  Pallas kernels: 34.3 us -> 32.6 us
    pallas_call x1, Pallas kernels: 32.6 us -> 30.8 us  [local_step(): pl.pallas_call(functools.partial(body, images, tokens, dim, heads, n), ou...]
where the time goes in v2:
time: 33.5 us; the launch traced here: 33.4 us
  Pallas kernels  32.6 us (97%)
  between operations  0.8 us (2%)
    pallas_call x1, Pallas kernels, local_step(): pl.pallas_call(functools.partial(body, images, tokens, dim, heads, n), ou...  30.8 us
    pallas_call x1, Pallas kernels, local_step(): pl.pallas_call(functools.partial(finish, dim, heads), out_shape=(jax.Shap...  1.76 us

profile of v2, /device:TPU:0, one launch (start us, length us, event | category | flops | bytes accessed | tf_op | source)
XLA Modules:
  0.0 33.4 jit_solution(14080494774253618209)
XLA Ops:
  0.6 30.8 %xca_step.1 = (bf16[2048,384]{1,0:T(8,128)(2,1)S(1)}, bf16[2048,384]{1,0:T(8,128)(2,1)S(1)}, bf16[48,1152]{1,0:T(8,128)(2,1)S(1)}, bf16[48,384]{1,0:T(8,128)(2,1)S(1)}, f32[8,128]{1,0:T(8,128)S(1)}) custom-call(bf16[2,1024,384]{2,1,0:T(8,128)(2,1)} %x_hbm.1, bf16[2,1024,384]{2,1,0:T(8,128)(2,1)} %dy_hbm.1, f32[384]{0:T(512)} %gain_hbm.1, f32[384]{0:T(512)} %bias_hbm.1, ...), custom_call_target="tpu_custom_call" | custom-call | tf_op jit(solution)/shard_map/xca_step/pallas_call | solution.py:581
  31.5 1.8 %xca_finish.1 = (bf16[2048,384]{1,0:T(8,128)(2,1)}, bf16[2048,384]{1,0:T(8,128)(2,1)}, bf16[48,1152]{1,0:T(8,128)(2,1)}, bf16[48,384]{1,0:T(8,128)(2,1)}, f32[384]{0:T(512)}, /*index=5*/f32[384]{0:T(512)}, f32[8]{0:T(128)}) custom-call(bf16[2048,384]{1,0:T(8,128)(2,1)S(1)} %get-tuple-element.19.y_v, bf16[2048,384]{1,0:T(8,128)(2,1)S(1)} %get-tuple-element.20.dx_v, ...), custom_call_target="tpu_custom_call" | custom-call | tf_op jit(solution)/shard_map/xca_finish/pallas_call | solution.py:640

commit v3 on v2

--- a/solution.py
+++ b/solution.py
@@ -342,12 +342,15 @@
     def rs0(c):
         pair_copy(c).start()
 
-    def rs1(c):
-        with scope("wait_pair"):
-            pair_copy(c).wait_recv()
-        chip_sum[:, :, :, :, cols(c)] = part[:, :, core, :, :, cols(c)] + pair_recv[:, :, :, :, cols(c)]
-        for stage in (FAR, NEAR):
-            for copy in stage_copies(c, stage):
+    def rs1(*chunks):
+        for c in chunks:
+            with scope("wait_pair"):
+                pair_copy(c).wait_recv()
+            chip_sum[:, :, :, :, cols(c)] = part[:, :, core, :, :, cols(c)] + pair_recv[:, :, :, :, cols(c)]
+            for copy in stage_copies(c, FAR):
+                copy.start()
+        for c in chunks:
+            for copy in stage_copies(c, NEAR):
                 copy.start()
 
     def rs2(c):
@@ -460,42 +463,41 @@
     with scope("group3"):
         part_qkv(0, 0)
         grad_v(1)
-    rs1(0)
-    with scope("group3b"):
         part_qkv(1, 0)
         rs0(1)
+    rs1(0)
     build_g(0)
     with scope("group4"):
         grad_q(0)
         part_qkv(0, 1)
+        grad_k(0)
     build_g(1)
+    with scope("group4b"):
+        grad_q(1)
     rs1(1)
     with scope("group5"):
-        grad_q(1)
         part_qkv(1, 1)
         rs0(2)
-        grad_k(0)
         grad_k(1)
         part_qkv(0, 2)
-    rs1(2)
     rs2(0)
     with scope("group6"):
         part_qkv(1, 2)
         rs0(3)
         rs0(4)
-    with scope("out_y"):
+    rs1(2)
+    ln_sums = []
+    with scope("group7"):
         out_y(0)
         out_y(1)
-    rs1(3)
-    rs1(4)
+    rs1(3, 4)
     rs2(1)
-    ln_sums = []
-    with scope("group7"):
+    with scope("group8"):
         ln_sums.append(grad_u(0, 0))
         ln_sums.append(grad_u(0, 1))
         ln_sums.append(grad_u(1, 0))
     rs2(2)
-    with scope("group8"):
+    with scope("group8b"):
         ln_sums.append(grad_u(1, 1))
 
     sg = sum(val[0] for val in ln_sums)

time: 33.5 us -> 32.5 us (0.970)
  Pallas kernels: 32.6 us -> 31.6 us
    pallas_call x1, Pallas kernels: 30.8 us -> 29.9 us  [local_step(): pl.pallas_call(functools.partial(body, images, tokens, dim, heads, n), ou...]
where the time goes in v3:
time: 32.5 us; the launch traced here: 32.4 us
  Pallas kernels  31.6 us (97%)
  between operations  0.8 us (2%)
    pallas_call x1, Pallas kernels, local_step(): pl.pallas_call(functools.partial(body, images, tokens, dim, heads, n), ou...  29.9 us
    pallas_call x1, Pallas kernels, local_step(): pl.pallas_call(functools.partial(finish, dim, heads), out_shape=(jax.Shap...  1.76 us

profile of v3, /device:TPU:0, one launch (start us, length us, event | category | flops | bytes accessed | tf_op | source)
XLA Modules:
  0.0 32.4 jit_solution(1355462096826205426)
XLA Ops:
  0.6 29.9 %xca_step.1 = (bf16[2048,384]{1,0:T(8,128)(2,1)S(1)}, bf16[2048,384]{1,0:T(8,128)(2,1)S(1)}, bf16[48,1152]{1,0:T(8,128)(2,1)S(1)}, bf16[48,384]{1,0:T(8,128)(2,1)S(1)}, f32[8,128]{1,0:T(8,128)S(1)}) custom-call(bf16[2,1024,384]{2,1,0:T(8,128)(2,1)} %x_hbm.1, bf16[2,1024,384]{2,1,0:T(8,128)(2,1)} %dy_hbm.1, f32[384]{0:T(512)} %gain_hbm.1, f32[384]{0:T(512)} %bias_hbm.1, ...), custom_call_target="tpu_custom_call" | custom-call | tf_op jit(solution)/shard_map/xca_step/pallas_call | solution.py:583
  30.5 1.8 %xca_finish.1 = (bf16[2048,384]{1,0:T(8,128)(2,1)}, bf16[2048,384]{1,0:T(8,128)(2,1)}, bf16[48,1152]{1,0:T(8,128)(2,1)}, bf16[48,384]{1,0:T(8,128)(2,1)}, f32[384]{0:T(512)}, /*index=5*/f32[384]{0:T(512)}, f32[8]{0:T(128)}) custom-call(bf16[2048,384]{1,0:T(8,128)(2,1)S(1)} %get-tuple-element.19.y_v, bf16[2048,384]{1,0:T(8,128)(2,1)S(1)} %get-tuple-element.20.dx_v, ...), custom_call_target="tpu_custom_call" | custom-call | tf_op jit(solution)/shard_map/xca_finish/pallas_call | solution.py:642

commit v4 on v3

--- a/solution.py
+++ b/solution.py
@@ -55,6 +55,10 @@
     dev_x = me + 2 - 4 * px
     dev_y = me + 4 - 8 * py
 
+    dev_d = 6 + 2 * core - me
+    other = 1 - 2 * core
+    peers = (dev_d, dev_d + other, dev_x, dev_y, dev_x + other, dev_y + other, partner)
+
     def dev(d):
         return {"sp": d}
 
@@ -86,7 +90,7 @@
 
     barrier = pltpu.get_barrier_semaphore()
     for off in range(1, n):
-        pl.semaphore_signal(barrier, inc=1, device_id=dev(lax.rem(me + off, n)), device_id_type=MESH)
+        pl.semaphore_signal(barrier, inc=1, device_id=dev(peers[off - 1]), device_id_type=MESH)
 
     lane = lax.broadcasted_iota(jnp.int32, (hd, LANES), 1)
     row = lax.broadcasted_iota(jnp.int32, (hd, LANES), 0)
@@ -136,7 +140,7 @@
             src_ref=ref, dst_ref=ref, send_sem=ssem, recv_sem=rsem, device_id=dev(partner), device_id_type=MESH)
 
     def exchange(send, recv, ssem, rsem, b, off):
-        dst = lax.rem(me + off, n)
+        dst = peers[off - 1]
         return pltpu.make_async_remote_copy(
             src_ref=send.at[b, dst], dst_ref=recv.at[b, off - 1],
             send_sem=ssem, recv_sem=rsem.at[b], device_id=dev(dst), device_id_type=MESH)
@@ -150,7 +154,7 @@
     def spread(buf, ssem, rsem, b, off):
         return pltpu.make_async_remote_copy(
             src_ref=buf.at[b, me], dst_ref=buf.at[b, me], send_sem=ssem, recv_sem=rsem.at[b],
-            device_id=dev(lax.rem(me + off, n)), device_id_type=MESH)
+            device_id=dev(peers[off - 1]), device_id_type=MESH)
 
     def a_copy(b, off):
         return spread(back_a, a_ssem, a_rsem, b, off)
@@ -509,7 +513,7 @@
     def ln_copy(off):
         return pltpu.make_async_remote_copy(
             src_ref=ln_all.at[me], dst_ref=ln_all.at[me], send_sem=ln_ssem, recv_sem=ln_rsem,
-            device_id=dev(lax.rem(me + off, n)), device_id_type=MESH)
+            device_id=dev(peers[off - 1]), device_id_type=MESH)
 
     for off in range(1, n):
         ln_copy(off).start()

time: 32.5 us -> 32.5 us (level)
  no operation moved by 1% of the time
where the time goes in v4:
time: 32.5 us; the launch traced here: 32.4 us
  Pallas kernels  31.6 us (97%)
  between operations  0.8 us (2%)
    pallas_call x1, Pallas kernels, local_step(): pl.pallas_call(functools.partial(body, images, tokens, dim, heads, n), ou...  29.9 us
    pallas_call x1, Pallas kernels, local_step(): pl.pallas_call(functools.partial(finish, dim, heads), out_shape=(jax.Shap...  1.76 us

profile of v4, /device:TPU:0, one launch (start us, length us, event | category | flops | bytes accessed | tf_op | source)
XLA Modules:
  0.0 32.4 jit_solution(9820801059667372282)
XLA Ops:
  0.6 29.9 %xca_step.1 = (bf16[2048,384]{1,0:T(8,128)(2,1)S(1)}, bf16[2048,384]{1,0:T(8,128)(2,1)S(1)}, bf16[48,1152]{1,0:T(8,128)(2,1)S(1)}, bf16[48,384]{1,0:T(8,128)(2,1)S(1)}, f32[8,128]{1,0:T(8,128)S(1)}) custom-call(bf16[2,1024,384]{2,1,0:T(8,128)(2,1)} %x_hbm.1, bf16[2,1024,384]{2,1,0:T(8,128)(2,1)} %dy_hbm.1, f32[384]{0:T(512)} %gain_hbm.1, f32[384]{0:T(512)} %bias_hbm.1, ...), custom_call_target="tpu_custom_call" | custom-call | tf_op jit(solution)/shard_map/xca_step/pallas_call | solution.py:587
  30.5 1.8 %xca_finish.1 = (bf16[2048,384]{1,0:T(8,128)(2,1)}, bf16[2048,384]{1,0:T(8,128)(2,1)}, bf16[48,1152]{1,0:T(8,128)(2,1)}, bf16[48,384]{1,0:T(8,128)(2,1)}, f32[384]{0:T(512)}, /*index=5*/f32[384]{0:T(512)}, f32[8]{0:T(128)}) custom-call(bf16[2048,384]{1,0:T(8,128)(2,1)S(1)} %get-tuple-element.19.y_v, bf16[2048,384]{1,0:T(8,128)(2,1)S(1)} %get-tuple-element.20.dx_v, ...), custom_call_target="tpu_custom_call" | custom-call | tf_op jit(solution)/shard_map/xca_finish/pallas_call | solution.py:646
